TPU v7x, 256 devices: a whole 4x4x8 slice. The times are simulated.
256 devices in a mesh: row: 32 (over x_hi, z, core), ga: 8 (over x_lo, y).
Axes of the slice: x: 4 (x_hi: 2, x_lo: 2; x = x_hi * 2 + x_lo), y: 4, z: 8, core: 2. Of those that a mesh axis runs over, the one named last changes fastest.
Arguments:
- pair_dens: bfloat16 [32, 256, 4096], P('row', None, 'ga'), may hold values from -0.41992188 to 0.41992188
- cond_dens: bfloat16 [32, 1024, 4096], P('row', None, 'ga'), may hold values from -0.41992188 to 0.41992188
- val_dens: bfloat16 [32, 64, 4096], P(None, None, 'row'), may hold values from -0.41992188 to 0.41992188
- screened: bfloat16 [8, 4096, 4096], P(None, 'ga', 'row'), may hold values from -1 to 6, as said below
- coulomb: bfloat16 [4096], P('ga'), may hold values from 0.29882812 to 10
- pair_list: int32 [32, 256], replicated, may hold values from 0 to 255, each once within a row
- counts: int32 [32], replicated, may hold values from 10 to 256
- q_index: int32 [32], replicated, may hold values from 0 to 7
- column_k: int32 [1], replicated, may hold values from 0 to 31
Outputs:
- kernel: bfloat16 [8192, 256], P('row', 'ga')
Inputs may be any that keep to these rules, and one draw needn't show every extreme that they name: `screened`: each diagonal entry exceeds the sum of the magnitudes of the others in its row divided by the square root of 4096 times four.
All inputs are finite; a program needn't handle non-finite values.
Results may differ from a plain program's by a relative error of at most 0.0042.
Values may be sent and summed in bfloat16 or wider, within the bound.
A program may use at most 64 MiB of HBM per device.

v0:
```python
import jax
import jax.numpy as jnp
from jax import lax
from jax.sharding import PartitionSpec as P

NV = 8
NC = 32


def picked(shard, axis, root):
    return lax.dynamic_index_in_dim(lax.all_gather(shard, axis), root, 0, keepdims=False)


def split_up(shard, dim, devices):
    lengths = shard.shape
    parts = shard.reshape(*lengths[:dim], devices, lengths[dim] // devices, *lengths[dim + 1 :])
    return jnp.moveaxis(parts, dim, 0)


def sum_at_owner(shard, axis, dim):
    devices = lax.axis_size(axis)
    parts = lax.all_to_all(split_up(shard, dim, devices), axis, 0, 0, tiled=True)
    return jnp.sum(parts.astype(jnp.float32), axis=0)


def sum_at_owner_2(shard, axis, dim):
    parts = split_up(shard, dim, lax.axis_size(axis))
    arrived = lax.all_to_all(parts, axis, split_axis=0, concat_axis=0, tiled=True)
    return arrived.sum(axis=0)


def per_device(
    pair_dens, cond_dens, val_dens, screened, coulomb, pair_list, counts, q_index, column_k
):
    kdev = pair_dens.shape[0]
    slots_all = pair_dens.shape[1]
    mine = lax.axis_index("row")
    column = column_k[0]
    root = column // kdev
    local_slot = column % kdev
    own_col = lax.dynamic_index_in_dim(pair_dens, local_slot, 0, keepdims=False)
    col_full = picked(own_col, "row", root)
    col_pairs = pair_list[column]
    col = jnp.take(col_full, col_pairs, axis=0)
    first = mine * kdev
    my_pairs = lax.dynamic_slice_in_dim(pair_list, first, kdev, 0)
    my_counts = lax.dynamic_slice_in_dim(counts, first, kdev, 0)
    blocks = jnp.take(screened, q_index, axis=0)
    screened_val = sum_at_owner(
        jnp.einsum("kvg,khg->kvh", val_dens, blocks, preferred_element_type=jnp.float32).astype(
            jnp.bfloat16
        ),
        "row",
        0,
    )
    screened_val = screened_val.astype(jnp.bfloat16)
    direct_full = jnp.einsum(
        "kag,kvg->kav", cond_dens, screened_val, preferred_element_type=jnp.float32
    )
    arranged = (
        direct_full.reshape(kdev, NC, NC, NV, NV)
        .transpose(0, 3, 1, 4, 2)
        .reshape(kdev, slots_all, slots_all)
    )
    direct = jnp.take(
        jnp.take_along_axis(arranged, my_pairs[:, :, None], axis=1), col_pairs, axis=2
    )
    rows = jnp.take_along_axis(pair_dens, my_pairs[:, :, None], axis=1)
    weighted = (rows.astype(jnp.float32) * coulomb.astype(jnp.float32)[None, None, :]).astype(
        jnp.bfloat16
    )
    exch = jnp.einsum("ksg,tg->kst", weighted, col, preferred_element_type=jnp.float32)
    slot_ids = jnp.arange(slots_all, dtype=jnp.int32)
    row_mask = (slot_ids[None, :] < my_counts[:, None]).astype(jnp.float32)
    col_mask = (slot_ids < counts[column]).astype(jnp.float32)
    masking = row_mask[:, :, None] * col_mask[None, None, :]
    combined = ((2.0 * exch - direct) * masking).reshape(kdev * slots_all, slots_all)
    summed = sum_at_owner_2(combined, "ga", 1)
    return summed.astype(jnp.bfloat16)


def solution(mesh):
    placed = (
        P("row", None, "ga"),
        P("row", None, "ga"),
        P(None, None, "row"),
        P(None, "ga", "row"),
        P("ga"),
        P(),
        P(),
        P(),
        P(),
    )
    return jax.shard_map(
        per_device, mesh=mesh, in_specs=placed, out_specs=P("row", "ga"), check_vma=False
    )
```

profile of v0, /device:TPU:1, one launch (start us, length us, event | category | flops | bytes accessed | tf_op | source)
XLA Modules:
  0.0 152.6 jit_solution(6338403845606772508)
XLA Ops:
  6.5 0.0 copy-start
  6.5 0.0 all-gather.2.cloned.1.call-start
  6.5 0.7 all-gather.2.cloned.1.call-update
  7.3 0.7 compare_select_fusion.4
  7.9 0.0 copy-done
  7.9 0.0 copy-start.6
  7.9 0.0 copy-start.5
  8.0 3.1 %gather_fusion.2 = bf16[32,512,128]{2,1,0:T(8,128)(2,1)} fusion(bf16[8,512,128]{2,1,0:T(8,128)(2,1)S(1)} %copy-done, s32[1024]{0:T(1024)S(1)} %pad_clamp_fusion), kind=kCustom, calls=%fused_computation.2 | custom fusion | bytes 8388736 | tf_op jit(solution)/shard_map/jit(_take)/gather | solution.py:48
  11.0 0.0 copy-done.6
  11.0 0.0 copy-done.5
  11.0 0.0 copy-start.4
  11.0 0.0 copy-start.1
  11.1 5.2 %convert_bitcast_fusion = bf16[32,1,64,512]{3,2,1,0:T(8,128)(2,1)} fusion(bf16[32,64,128]{2,1,0:T(8,128)(2,1)S(1)} %copy-done.5, bf16[32,512,128]{2,1,0:T(8,128)(2,1)} %gather_fusion.2, pred[32]{0:T(512)(128)(4,1)S(1)} %compare_and_fusion), kind=kOutput, calls=%fused_computation.8 | convolution fusion | flops 271581184 | bytes 6815776 | tf_op jit(solution)/shard_map/kvg,khg->kvh/dot_general | solution.py:50
  16.3 0.0 copy-start.3
  16.3 12.7 %all-to-all-start = ((bf16[32,1,64,512]{3,2,1,0:T(8,128)(2,1)}), bf16[32,1,64,512]{3,2,1,0:T(8,128)(2,1)S(1)}, u32[]{:S(2)}, u32[]{:S(2)}) async-start(bf16[32,1,64,512]{3,2,1,0:T(8,128)(2,1)} %convert_bitcast_fusion), calls=%async_computation | async-start | bytes 4194304 | tf_op jit(solution)/shard_map/all_to_all | solution.py:22
  29.6 0.0 copy-done.4
  29.7 0.8 compare_select_fusion
  30.5 0.0 copy-done.1
  30.5 1.9 %gather_fusion = bf16[256,512]{1,0:T(8,128)(2,1)} fusion(bf16[256,512]{1,0:T(8,128)(2,1)S(1)} %bitcast.54, s32[1024]{0:T(1024)S(1)} %pad_clamp_fusion.2), kind=kCustom, calls=%fused_computation | custom fusion | bytes 525312 | tf_op jit(solution)/shard_map/jit(take_along_axis)/gather | solution.py:68
  32.4 0.0 copy-done.3
  32.4 0.7 fusion.18
  33.0 1.3 compare_convert_fusion
  34.4 55.6 %all-to-all-done = bf16[32,1,64,512]{3,2,1,0:T(8,128)(2,1)S(1)} async-done(((bf16[32,1,64,512]{3,2,1,0:T(8,128)(2,1)}), bf16[32,1,64,512]{3,2,1,0:T(8,128)(2,1)S(1)}, u32[]{:S(2)}, u32[]{:S(2)}) %all-to-all-start) | async-done | bytes 2097184 | tf_op jit(solution)/shard_map/all_to_all | solution.py:22
  90.0 0.3 reduce_sum.21
  90.3 2.2 %convolution_bitcast_fusion = f32[1,8,32,8,32]{4,3,2,1,0:T(8,128)S(1)} fusion(bf16[32,32,512,1]{2,1,0,3:T(8,128)(2,1)} %bitcast.55, bf16[64,512]{1,0:T(8,128)(2,1)S(1)} %reduce_sum.21), kind=kOutput, calls=%fused_computation.10 | convolution fusion | flops 67108864 | bytes 1376256 | tf_op jit(solution)/shard_map/kag,kvg->kav/dot_general | solution.py:57
  92.5 0.3 reshape.233
  92.8 0.0 copy-start.2
  92.8 1.0 gather_fusion.3
  93.8 0.1 fusion.8
  93.9 0.1 copy.13
  94.0 1.0 gather_fusion.4
  95.0 37.4 %all-gather.2.cloned.1.call-done = bf16[32,256,512]{2,1,0:T(8,128)(2,1)} async-done(((bf16[1,256,512]{2,1,0:T(8,128)(2,1)}), bf16[32,256,512]{2,1,0:T(8,128)(2,1)}) %all-gather.2.cloned.1.call-update) | async-done | bytes 8388624 | tf_op jit(solution)/shard_map/all_gather | solution.py:11
  132.4 1.0 dynamic-slice_bitcast_fusion
  133.4 1.2 gather_fusion.1
  134.5 0.0 copy-done.2
  134.6 0.4 fusion.7
  134.9 10.2 %all_to_all.10 = f32[8,256,32]{1,2,0:T(8,128)S(1)} all-to-all(f32[8,256,32]{1,2,0:T(8,128)S(1)} %bitcast.56), channel_id=1, replica_groups=mesh['row'=32,'ga'=8] {'ga'}, dimensions={0} | all-to-all | bytes 524288 | tf_op jit(solution)/shard_map/all_to_all | solution.py:28
  145.1 0.6 reduce_sum.22
  (6 shorter events, 0.0 us)
Async XLA Ops:
  6.5 1.4 copy-start
  6.5 125.9 %all-gather.2.cloned.1.call-start = ((), (), s32[]{:S(2)}) async-start(), calls=%async_computation.2 | async-start | bytes 8650752 | tf_op jit(solution)/shard_map/all_gather | solution.py:11
  7.9 3.1 %copy-start.6 = (s32[32]{0:T(128)S(1)}, s32[32]{0:T(128)}, u32[]{:S(2)}) copy-start(s32[32]{0:T(128)} %param.16) | copy-start | bytes 388
  7.9 3.1 %copy-start.5 = (bf16[32,64,128]{2,1,0:T(8,128)(2,1)S(1)}, bf16[32,64,128]{2,1,0:T(8,128)(2,1)}, u32[]{:S(2)}) copy-start(bf16[32,64,128]{2,1,0:T(8,128)(2,1)} %param.11) | copy-start | bytes 1572868
  11.0 18.6 %copy-start.4 = (bf16[512]{0:T(512)(128)(2,1)S(1)}, bf16[512]{0:T(512)(128)(2,1)}, u32[]{:S(2)}) copy-start(bf16[512]{0:T(512)(128)(2,1)} %param.13) | copy-start | bytes 3076
  11.0 19.4 %copy-start.1 = (bf16[1,256,512]{2,1,0:T(8,128)(2,1)S(1)}, bf16[1,256,512]{2,1,0:T(8,128)(2,1)}, u32[]{:S(2)}) copy-start(bf16[1,256,512]{2,1,0:T(8,128)(2,1)} %param.9) | copy-start | bytes 786436
  16.3 16.1 %copy-start.3 = (s32[32]{0:T(128)S(1)}, s32[32]{0:T(128)}, u32[]{:S(2)}) copy-start(s32[32]{0:T(128)} %param.15) | copy-start | bytes 388
  16.3 73.7 %all-to-all-start = ((bf16[32,1,64,512]{3,2,1,0:T(8,128)(2,1)}), bf16[32,1,64,512]{3,2,1,0:T(8,128)(2,1)S(1)}, u32[]{:S(2)}, u32[]{:S(2)}) async-start(bf16[32,1,64,512]{3,2,1,0:T(8,128)(2,1)} %convert_bitcast_fusion), calls=%async_computation | async-start | bytes 4194304 | tf_op jit(solution)/shard_map/all_to_all | solution.py:22
  92.8 41.8 %copy-start.2 = (bf16[256,512]{1,0:T(8,128)(2,1)S(1)}, bf16[256,512]{1,0:T(8,128)(2,1)}, u32[]{:S(2)}) copy-start(bf16[256,512]{1,0:T(8,128)(2,1)} %gather_fusion) | copy-start | bytes 786436
Sparse Core Ops, SparseCore 0:
  10.1 122.2 all-gather.1
where the time goes:
time: 153 us
  waiting for transfers between devices  93.7 us (61%)
  between operations  14.2 us (9%)
  starting transfers between devices  12.7 us (8%)
  local copies, waits for them, and re-layouts  10.2 us (7%)
  blocking collectives  10.2 us (7%)
  matrix products  7.76 us (5%)
  other arithmetic  3.85 us (3%)
    all_to_all x1, waiting for transfers between devices, sum_at_owner(): lax.all_to_all(split_up(shard, dim, devices), axis, 0, 0, tiled=True)  55.6 us
    all_gather x1, waiting for transfers between devices, picked(): lax.all_gather(shard, axis)  37.4 us
    all_to_all x1, starting transfers between devices, sum_at_owner(): lax.all_to_all(split_up(shard, dim, devices), axis, 0, 0, tiled=True)  12.7 us
    all_to_all x1, blocking collectives, sum_at_owner_2(): lax.all_to_all(parts, axis, split_axis=0, concat_axis=0, tiled=True)  10.2 us
    dot_general x1, matrix products, per_device(): jnp.einsum('kvg,khg->kvh', val_dens, blocks, preferred_element_type=jnp.f...  5.22 us
  transfers between devices with their start and end apart: 2, of which 2 were waited for; matrix products, arithmetic and copies ran while one was open for 12% of the time, Pallas kernels for 0%

commit v1 on v0

v1 whole, which is shorter than its diff:
```python
import jax
import jax.numpy as jnp
from jax import lax
from jax.experimental import pallas as pl
from jax.experimental.pallas import tpu as pltpu
from jax.sharding import PartitionSpec as P

NV = 8
NC = 32
F32 = jnp.float32
BF16 = jnp.bfloat16
MESH = pl.DeviceIdType.MESH

ORDER = (4, 3, 5, 2, 6, 1, 7, 0)


def dot_t(a, b):
    return lax.dot_general(a, b, (((1,), (1,)), ((), ())), preferred_element_type=F32)


def dot_l(a, b):
    return lax.dot_general(a, b, (((0,), (0,)), ((), ())), preferred_element_type=F32)


def one_hot(condition):
    return jnp.where(condition, 1.0, 0.0).astype(BF16)


def iota(shape, dim):
    return lax.broadcasted_iota(jnp.int32, shape, dim)


def kernel(
    counts, q_index, column_k, pairs, coulomb, pd_hbm, cond_hbm, val_hbm, scr_hbm, out_ref,
    pd, cond, val, scr, own, obuf, orecv, zsend, zrecv, xsend, xrecv, mine_sum,
    cgb, c0buf, cand, c1buf, colbuf, perm, wperm, pick, exch, gsend, grecv,
    load_sem, o_s, o_r, z_s, z_r, x_s, x_r, c0_s, c0_r, c1_s, c1_r, c2_s, c2_r, c3_s, c3_r, g_s, g_r,
):
    row = lax.axis_index("row")
    ga = lax.axis_index("ga")
    core = row % 2
    z = (row // 2) % 8
    h = row // 16
    sent = []

    def at(hh, zz, cc):
        return {"row": (hh * 8 + zz) * 2 + cc, "ga": ga}

    def send(src, dst, s, r, where):
        copy = pltpu.make_async_remote_copy(
            src_ref=src, dst_ref=dst, send_sem=s, recv_sem=r, device_id=where, device_id_type=MESH
        )
        copy.start()
        sent.append(copy)
        return copy

    partner = at(h, z, 1 - core)
    far = at(1 - h, z, core)
    chips = [(dh, dz) for dz in (4, 3, 5, 2, 6, 1, 7, 0) for dh in (1, 0) if (dh, dz) != (0, 0)]

    loads = [
        pltpu.make_async_copy(src, dst, load_sem.at[i])
        for i, (src, dst) in enumerate(
            ((pd_hbm.at[0], pd), (val_hbm, val), (scr_hbm, scr), (cond_hbm.at[0], cond))
        )
    ]
    for load in loads:
        load.start()

    barrier = pltpu.get_barrier_semaphore()
    peers = [partner] + [at((h + dh) % 2, (z + dz) % 8, core) for dh, dz in chips]
    peers += [{"row": row, "ga": (ga + d) % 8} for d in range(1, 8)]
    for peer in peers:
        pl.semaphore_signal(barrier, inc=1, device_id=peer, device_id_type=MESH)

    ck = column_k[0]
    root_h = ck // 16
    root_z = (ck // 2) % 8
    root_core = ck % 2
    cp = pairs[pl.ds(ck, 1), :]

    loads[0].wait()
    gather = one_hot(iota((256, 256), 0) == cp)
    cg = dot_l(gather, pd[...]).astype(BF16)
    for c in range(2):
        for s in range(2):
            cgb[c, s] = cg[c * 128 : c * 128 + 128, s * 256 : s * 256 + 256].reshape(8, 16, 256)

    loads[1].wait()
    loads[2].wait()

    def product(side, dz, cc):
        k = (((h + 1 - side) % 2) * 8 + (z + dz) % 8) * 2 + cc
        return dot_t(val[k], scr[q_index[k]])

    def others(dz):
        for side in range(2):
            obuf[dz, side] = product(side, dz, 1 - core).astype(BF16)

    o_copies = {}

    def send_others(dz):
        o_copies[dz] = send(obuf.at[dz], orecv.at[dz], o_s.at[dz], o_r.at[dz], partner)

    def mine(dz):
        o_copies[dz].wait_recv()
        for side in range(2):
            own[dz, side] = product(side, dz, core) + orecv[dz, side].astype(F32)

    z_copies = {}

    def half(w):
        return pl.ds(w * 32, 32)

    def z_send(d, side, slot, value):
        zsend[d, side, slot] = value.astype(BF16)
        z_copies[d, side, slot] = send(
            zsend.at[d, side, slot], zrecv.at[d, side, slot], z_s.at[d, side, slot], z_r.at[d, side, slot],
            at(h, (z + (1, 7)[d]) % 8, core),
        )

    def z_got(d, side, slot):
        z_copies[d, side, slot].wait_recv()
        return zrecv[d, side, slot].astype(F32)

    others(4)
    others(3)
    others(5)
    pl.semaphore_wait(barrier, len(peers))
    c0 = send(cgb.at[1 - core], c0buf, c0_s, c0_r, partner)
    for dz in (4, 3, 5):
        send_others(dz)
    for dz in ORDER[3:]:
        others(dz)
        send_others(dz)

    c0.wait_recv()
    cand[...] = jnp.where(root_core == core, cgb[core], c0buf[...])
    c1 = []
    for i, (dh, dz) in enumerate(chips):
        hh, zz = (h + dh) % 2, (z + dz) % 8
        c1.append(send(cand.at[hh, zz], c1buf.at[h, z], c1_s.at[i], c1_r.at[i], at(hh, zz, core)))
    c1buf[h, z] = cand[h, z]

    mine(4)
    for side in range(2):
        z_send(0, side, 0, own[4, side, half(0), :])
        z_send(1, side, 0, own[4, side, half(1), :])
    mine(3)
    for side in range(2):
        z_send(0, side, 1, own[3, side, half(1), :])
    mine(5)
    for side in range(2):
        z_send(1, side, 1, own[5, side, half(0), :])
    for dz in ORDER[3:]:
        mine(dz)

    def relay(slot):
        for side in range(2):
            for d in range(2):
                dz = (4 - (slot + 1) // 2) * (1, 7)[d] % 8
                first_half = slot % 2 == 0
                w = d if first_half else 1 - d
                z_send(d, side, slot, own[dz, side, half(w), :] + z_got(d, side, slot - 2))

    relay(2)
    relay(3)

    wt = (pd[...].astype(F32) * coulomb[...].astype(F32)).astype(BF16)
    r0, p0 = iota((256, 256), 0), iota((256, 256), 1)
    order = one_hot(p0 == (r0 % 8) * 32 + ((r0 // 8) % 8) * 4 + r0 // 64)
    wperm[...] = jnp.dot(order, wt, preferred_element_type=F32).astype(BF16)
    kp = pairs[pl.ds(row, 1), :]
    kc = kp % 32
    target = (kc % 4) * 64 + (kc // 4) * 8 + kp // 32
    perm[...] = jnp.transpose(
        jnp.where((r0 == target) & (p0 < counts[row]), 1.0, 0.0).astype(F32)
    ).astype(BF16)
    i0 = iota((128, 256), 0)
    for j in range(4):
        pick[j] = one_hot((i0 // 32 == j) & (i0 % 32 == cp % 32))

    relay(4)

    for copy in c1:
        copy.wait_recv()
    colbuf[h, core, z] = c1buf[root_h, root_z]
    c2 = []
    for i, (dh, dz) in enumerate(chips):
        mine_slot = colbuf.at[h, core, z]
        c2.append(send(mine_slot, mine_slot, c2_s.at[i], c2_r.at[i], at((h + dh) % 2, (z + dz) % 8, core)))

    relay(5)
    relay(6)

    x_copies = []
    for w in range(2):
        total = own[0, 0, half(w), :] + z_got(w, 0, 6) + z_got(1 - w, 0, 5)
        xsend[w] = total.astype(BF16)
        x_copies.append(send(xsend.at[w], xrecv.at[w], x_s.at[w], x_r.at[w], far))
    for w in range(2):
        mine_sum[half(w), :] = own[0, 1, half(w), :] + z_got(w, 1, 6) + z_got(1 - w, 1, 5)

    for copy in c2:
        copy.wait_recv()
    c3 = []
    for s in range(2):
        c3.append(send(colbuf.at[s, core], colbuf.at[s, core], c3_s.at[s], c3_r.at[s], partner))
    for copy in c3:
        copy.wait_recv()
    exch[...] = 2.0 * (
        dot_t(wperm[:, 0:256], colbuf[0].reshape(256, 256))
        + dot_t(wperm[:, 256:512], colbuf[1].reshape(256, 256))
    )

    loads[3].wait()
    for copy in x_copies:
        copy.wait_recv()
    sv = (mine_sum[...] + xrecv[...].reshape(64, 512).astype(F32)).astype(BF16)
    w0, w1 = iota((64, 64), 0), iota((64, 64), 1)
    swap = one_hot(w1 == (w0 % 8) * 8 + w0 // 8)
    sv = jnp.dot(swap, sv, preferred_element_type=F32).astype(BF16)
    dt = dot_t(sv, cond[...]).astype(BF16)
    dt = jnp.concatenate([dt[:, b * 128 : b * 128 + 128] for b in range(8)], axis=0)
    v_of = cp // 32
    parts = []
    for j in range(4):
        e = jnp.dot(dt, pick[j], preferred_element_type=F32).reshape(8, 8, 8, 256)
        total = jnp.where(v_of == 0, e[:, 0], 0.0)
        for v in range(1, 8):
            total = total + jnp.where(v_of == v, e[:, v], 0.0)
        parts.append(exch[j * 64 : j * 64 + 64, :] - total.reshape(64, 256))
    for d in range(8):
        piece = jnp.concatenate([p[:, d * 32 : d * 32 + 32] for p in parts], axis=1)
        gsend[d] = piece.astype(BF16)
    g_copies = []
    for d in range(1, 8):
        to = (ga + d) % 8
        g_copies.append(
            send(gsend.at[to], grecv.at[d - 1], g_s.at[d - 1], g_r.at[d - 1], {"row": row, "ga": to})
        )
    total = gsend[ga].astype(F32)
    for d, copy in enumerate(g_copies):
        copy.wait_recv()
        total = total + grecv[d].astype(F32)
    total = total.astype(BF16).astype(F32)
    stacked = jnp.concatenate(
        [total if j == 0 else pltpu.roll(total, 128 - 32 * j, 1) for j in range(4)], axis=0
    ).astype(BF16)
    result = jnp.dot(perm[...], stacked, preferred_element_type=F32)
    slot = ga * 32 + iota((256, 128), 1)
    result = jnp.where(slot < counts[ck], result, 0.0)
    out_ref[...] = result[:, 0:32].astype(BF16)
    for copy in sent:
        copy.wait_send()


def per_device(
    pair_dens, cond_dens, val_dens, screened, coulomb, pair_list, counts, q_index, column_k
):
    dma = pltpu.SemaphoreType.DMA
    smem = pl.BlockSpec(memory_space=pltpu.SMEM)
    vmem = pl.BlockSpec(memory_space=pltpu.VMEM)
    hbm = pl.BlockSpec(memory_space=pl.ANY)
    return pl.pallas_call(
        kernel,
        out_shape=jax.ShapeDtypeStruct((256, 32), BF16),
        in_specs=[smem, smem, smem, vmem, vmem, hbm, hbm, hbm, hbm],
        out_specs=vmem,
        scratch_shapes=[
            pltpu.VMEM((256, 512), BF16),
            pltpu.VMEM((1024, 512), BF16),
            pltpu.VMEM((32, 64, 128), BF16),
            pltpu.VMEM((8, 512, 128), BF16),
            pltpu.VMEM((8, 2, 64, 512), F32),
            pltpu.VMEM((8, 2, 64, 512), BF16),
            pltpu.VMEM((8, 2, 64, 512), BF16),
            pltpu.VMEM((2, 2, 7, 32, 512), BF16),
            pltpu.VMEM((2, 2, 7, 32, 512), BF16),
            pltpu.VMEM((2, 32, 512), BF16),
            pltpu.VMEM((2, 32, 512), BF16),
            pltpu.VMEM((64, 512), F32),
            pltpu.VMEM((2, 2, 8, 16, 256), BF16),
            pltpu.VMEM((2, 8, 16, 256), BF16),
            pltpu.VMEM((2, 8, 16, 256), BF16),
            pltpu.VMEM((2, 8, 16, 256), BF16),
            pltpu.VMEM((2, 2, 8, 16, 256), BF16),
            pltpu.VMEM((256, 256), BF16),
            pltpu.VMEM((256, 512), BF16),
            pltpu.VMEM((4, 128, 256), BF16),
            pltpu.VMEM((256, 256), F32),
            pltpu.VMEM((8, 64, 128), BF16),
            pltpu.VMEM((7, 64, 128), BF16),
            dma((4,)),
            dma((8,)), dma((8,)),
            dma((2, 2, 7)), dma((2, 2, 7)),
            dma((2,)), dma((2,)),
            dma, dma,
            dma((15,)), dma((15,)),
            dma((15,)), dma((15,)),
            dma((2,)), dma((2,)),
            dma((7,)), dma((7,)),
        ],
        compiler_params=pltpu.CompilerParams(
            collective_id=0, has_side_effects=True, vmem_limit_bytes=48 * 1024 * 1024
        ),
        name="bse_block",
    )(
        counts, q_index, column_k, pair_list, coulomb.reshape(1, -1),
        pair_dens, cond_dens, val_dens, screened,
    )


def solution(mesh):
    placed = (
        P("row", None, "ga"),
        P("row", None, "ga"),
        P(None, None, "row"),
        P(None, "ga", "row"),
        P("ga"),
        P(),
        P(),
        P(),
        P(),
    )
    return jax.shard_map(
        per_device, mesh=mesh, in_specs=placed, out_specs=P("row", "ga"), check_vma=False
    )
```

time: 153 us -> 48.1 us (0.31)
  the two profiles are of different devices: /device:TPU:1 before, /device:TPU:4 now
where the time goes in v1:
time: 48.1 us; the launch traced here: 47.8 us
  Pallas kernels  40.6 us (84%)
  local copies, waits for them, and re-layouts  6.55 us (14%)
  between operations  0.7 us (1%)
    pallas_call x1, Pallas kernels, per_device(): pl.pallas_call(kernel, out_shape=jax.ShapeDtypeStruct((256, 32), BF16), i...  40.6 us
    unnamed x16, local copies, waits for them, and re-layouts  5.85 us

profile of v1, /device:TPU:4, one launch (start us, length us, event | category | flops | bytes accessed | tf_op | source)
XLA Modules:
  0.0 47.8 jit_solution(4659860195313710546)
XLA Ops:
  0.0 0.0 copy-start.7
  0.7 0.0 copy-done.7
  0.7 0.0 copy-start.5
  0.7 0.0 copy-start.6
  0.7 0.6 %copy-done.5 = s32[32]{0:T(128)S(1)} copy-done((s32[32]{0:T(128)S(1)}, s32[32]{0:T(128)}, u32[]{:S(2)}) %copy-start.5) | copy-done | bytes 152
  1.3 0.0 copy-done.6
  1.4 0.0 copy-start
  1.4 1.2 %copy-done = bf16[1,1024,512]{2,1,0:T(8,128)(2,1)S(1)} copy-done((bf16[1,1024,512]{2,1,0:T(8,128)(2,1)S(1)}, bf16[1,1024,512]{2,1,0:T(8,128)(2,1)}, u32[]{:S(2)}) %copy-start) | copy-done | bytes 1048600
  2.6 0.0 copy-start.1
  2.6 1.2 %copy-done.1 = bf16[8,512,128]{2,1,0:T(8,128)(2,1)S(1)} copy-done((bf16[8,512,128]{2,1,0:T(8,128)(2,1)S(1)}, bf16[8,512,128]{2,1,0:T(8,128)(2,1)}, u32[]{:S(2)}) %copy-start.1) | copy-done | bytes 1048600
  3.8 0.0 copy-start.2
  3.8 1.0 %copy-done.2 = bf16[32,64,128]{2,1,0:T(8,128)(2,1)S(1)} copy-done((bf16[32,64,128]{2,1,0:T(8,128)(2,1)S(1)}, bf16[32,64,128]{2,1,0:T(8,128)(2,1)}, u32[]{:S(2)}) %copy-start.2) | copy-done | bytes 524312
  4.8 0.0 copy-start.3
  4.8 0.9 %copy-done.3 = bf16[1,256,512]{2,1,0:T(8,128)(2,1)S(1)} copy-done((bf16[1,256,512]{2,1,0:T(8,128)(2,1)S(1)}, bf16[1,256,512]{2,1,0:T(8,128)(2,1)}, u32[]{:S(2)}) %copy-start.3) | copy-done | bytes 262168
  5.8 0.0 copy-start.4
  5.8 0.8 %copy-done.4 = s32[32,256]{1,0:T(8,128)S(1)} copy-done((s32[32,256]{1,0:T(8,128)S(1)}, s32[32,256]{1,0:T(8,128)}, u32[]{:S(2)}) %copy-start.4) | copy-done | bytes 32792
  6.6 40.6 %bse_block.1 = bf16[256,32]{1,0:T(8,128)(2,1)S(1)} custom-call(s32[32]{0:T(128)S(1)} %copy-done.5, s32[32]{0:T(128)S(1)} %copy-done.6, s32[1]{0:T(128)S(6)} %copy.11.column_k, s32[32,256]{1,0:T(8,128)S(1)} %copy-done.4, bf16[1,512]{1,0:T(2,128)(2,1)S(1)} %reshape.3.coulomb, bf16[1,256,512]{2,1,0:T(8,128)(2,1)S(1)} %copy-done.3, ...), custom_call_target="tpu_custom_call" | custom-call | tf_op jit(solution)/shard_map/bse_block/pallas_call | solution.py:265
  47.1 0.7 %copy.10 = bf16[256,32]{0,1:T(8,128)(2,1)} copy(bf16[256,32]{1,0:T(8,128)(2,1)S(1)} %bse_block.1) | data formatting | bytes 32768 | tf_op jit(solution)/shard_map/bse_block/pallas_call | solution.py:265
  (1 shorter events, 0.0 us)
Async XLA Ops:
  0.0 0.7 %copy-start.7 = (bf16[512]{0:T(512)(128)(2,1)S(1)}, bf16[512]{0:T(512)(128)(2,1)}, u32[]{:S(2)}) copy-start(bf16[512]{0:T(512)(128)(2,1)} %param.13) | copy-start | bytes 3076
  0.7 0.7 %copy-start.5 = (s32[32]{0:T(128)S(1)}, s32[32]{0:T(128)}, u32[]{:S(2)}) copy-start(s32[32]{0:T(128)} %counts.1) | copy-start | bytes 388
  0.7 0.7 %copy-start.6 = (s32[32]{0:T(128)S(1)}, s32[32]{0:T(128)}, u32[]{:S(2)}) copy-start(s32[32]{0:T(128)} %q_index.1) | copy-start | bytes 388
  1.4 1.2 %copy-start = (bf16[1,1024,512]{2,1,0:T(8,128)(2,1)S(1)}, bf16[1,1024,512]{2,1,0:T(8,128)(2,1)}, u32[]{:S(2)}) copy-start(bf16[1,1024,512]{2,1,0:T(8,128)(2,1)} %cond_hbm.1) | copy-start | bytes 3145732
  2.6 1.2 %copy-start.1 = (bf16[8,512,128]{2,1,0:T(8,128)(2,1)S(1)}, bf16[8,512,128]{2,1,0:T(8,128)(2,1)}, u32[]{:S(2)}) copy-start(bf16[8,512,128]{2,1,0:T(8,128)(2,1)} %scr_hbm.1) | copy-start | bytes 3145732
  3.8 1.0 %copy-start.2 = (bf16[32,64,128]{2,1,0:T(8,128)(2,1)S(1)}, bf16[32,64,128]{2,1,0:T(8,128)(2,1)}, u32[]{:S(2)}) copy-start(bf16[32,64,128]{2,1,0:T(8,128)(2,1)} %val_hbm.1) | copy-start | bytes 1572868
  4.8 0.9 %copy-start.3 = (bf16[1,256,512]{2,1,0:T(8,128)(2,1)S(1)}, bf16[1,256,512]{2,1,0:T(8,128)(2,1)}, u32[]{:S(2)}) copy-start(bf16[1,256,512]{2,1,0:T(8,128)(2,1)} %pd_hbm.1) | copy-start | bytes 786436
  5.8 0.8 %copy-start.4 = (s32[32,256]{1,0:T(8,128)S(1)}, s32[32,256]{1,0:T(8,128)}, u32[]{:S(2)}) copy-start(s32[32,256]{1,0:T(8,128)} %pairs.1) | copy-start | bytes 98308

commit v2 on v1

v2 whole, which is shorter than its diff:
```python
import jax
import jax.numpy as jnp
from jax import lax
from jax.experimental import pallas as pl
from jax.experimental.pallas import tpu as pltpu
from jax.sharding import PartitionSpec as P

NV = 8
NC = 32
F32 = jnp.float32
BF16 = jnp.bfloat16
MESH = pl.DeviceIdType.MESH

ORDER = (4, 3, 5, 2, 6, 1, 7, 0)


def dot_t(a, b):
    return lax.dot_general(a, b, (((1,), (1,)), ((), ())), preferred_element_type=F32)


def dot_l(a, b):
    return lax.dot_general(a, b, (((0,), (0,)), ((), ())), preferred_element_type=F32)


def one_hot(condition):
    return jnp.where(condition, 1.0, 0.0).astype(BF16)


def iota(shape, dim):
    return lax.broadcasted_iota(jnp.int32, shape, dim)


def kernel(
    counts_hbm, q_hbm, column_hbm, pairs_hbm, coul_hbm, pd_hbm, cond_hbm, val_hbm, scr_hbm, out_ref,
    counts, q_index, column_k, pairs, coulomb, pd, cond, val, scr, own, obuf, orecv, zsend, zrecv, xb_from, xb_recv, xsend, xrecv, mine_sum,
    cgb, c0buf, cand, cxbuf, quarter, c1buf, colbuf, perm, wperm, pick, direct, gsend, grecv,
    load_sem, o_s, o_r, z_s, z_r, xb_s, xb_r, x_s, x_r, c0_s, c0_r, cx_s, cx_r, c1_s, c1_r, c2_s, c2_r, c3_s, c3_r, g_s, g_r, tokens,
):
    row = lax.axis_index("row")
    ga = lax.axis_index("ga")
    core = row % 2
    z = (row // 2) % 8
    h = row // 16
    sent = []

    def at(hh, zz, cc):
        return {"row": (hh * 8 + zz) * 2 + cc, "ga": ga}

    def send(src, dst, s, r, where):
        copy = pltpu.make_async_remote_copy(
            src_ref=src, dst_ref=dst, send_sem=s, recv_sem=r, device_id=where, device_id_type=MESH
        )
        copy.start()
        sent.append(copy)
        return copy

    partner = at(h, z, 1 - core)
    far = at(1 - h, z, core)
    chips = [(dh, dz) for dz in (4, 3, 5, 2, 6, 1, 7, 0) for dh in (1, 0) if (dh, dz) != (0, 0)]

    loads = [
        pltpu.make_async_copy(src, dst, load_sem.at[i])
        for i, (src, dst) in enumerate(
            (
                (column_hbm, column_k), (pairs_hbm, pairs), (q_hbm, q_index), (pd_hbm.at[0], pd),
                (val_hbm, val), (scr_hbm, scr), (cond_hbm.at[0], cond), (counts_hbm, counts), (coul_hbm, coulomb),
            )
        )
    ]
    for load in loads:
        load.start()

    barrier = pltpu.get_barrier_semaphore()
    near = [at(h, (z + d) % 8, core) for d in (1, 7, 2, 6)]
    near += [{"row": row, "ga": (ga // 4) * 4 + (ga + d) % 4} for d in (1, 3, 2)]
    near.append({"row": row, "ga": (ga + 4) % 8})
    for peer in near + [far, partner]:
        pl.semaphore_signal(barrier, inc=1, device_id=peer, device_id_type=MESH)

    loads[0].wait()
    loads[1].wait()
    ck = column_k[0]
    root_h = ck // 16
    root_z = (ck // 2) % 8
    root_core = ck % 2
    cp = pairs[pl.ds(ck, 1), :]

    loads[3].wait()
    gather = one_hot(iota((256, 256), 0) == cp)
    cg = dot_l(gather, pd[...]).astype(BF16)
    for c in range(2):
        for s in range(2):
            cgb[c, s] = cg[c * 128 : c * 128 + 128, s * 256 : s * 256 + 256].reshape(8, 16, 256)

    for load in (loads[2], loads[4], loads[5]):
        load.wait()

    def product(side, dz, cc):
        k = (((h + 1 - side) % 2) * 8 + (z + dz) % 8) * 2 + cc
        return dot_t(val[k], scr[q_index[k]])

    def others(dz):
        for side in range(2):
            obuf[dz, side] = product(side, dz, 1 - core).astype(BF16)

    o_copies = {}

    def send_others(dz):
        o_copies[dz] = send(obuf.at[dz], orecv.at[dz], o_s.at[dz], o_r.at[dz], partner)

    def mine(dz):
        o_copies[dz].wait_recv()
        for side in range(2):
            own[dz, side] = product(side, dz, core) + orecv[dz, side].astype(F32)

    z_copies = {}

    def part(unit, dz, q):
        if unit < 2:
            return own[dz, unit, pl.ds(q * 16, 16), :]
        return own[dz, 1, pl.ds(32 + q * 16, 16), :] + xb_recv[dz, pl.ds(q * 16, 16), :].astype(F32)

    def z_send(d, unit, slot, value):
        zsend[d, unit, slot] = value.astype(BF16)
        z_copies[d, unit, slot] = send(
            zsend.at[d, unit, slot], zrecv.at[d, unit, slot], z_s.at[d, unit, slot], z_r.at[d, unit, slot],
            at(h, (z + (1, 7)[d]) % 8, core),
        )

    def z_got(d, unit, slot):
        z_copies[d, unit, slot].wait_recv()
        return zrecv[d, unit, slot].astype(F32)

    def relay(unit, slot):
        for d in range(2):
            dz = (4 - (slot + 1) // 2) * (1, 7)[d] % 8
            q = d if slot % 2 == 0 else 1 - d
            value = part(unit, dz, q)
            if slot > 1:
                value = value + z_got(d, unit, slot - 2)
            z_send(d, unit, slot, value)

    def final(unit, q):
        return part(unit, 0, q) + z_got(q, unit, 6) + z_got(1 - q, unit, 5)

    xb_copies = {}

    def xb_send(dz):
        xb_from[dz] = own[dz, 0, pl.ds(32, 32), :].astype(BF16)
        xb_copies[dz] = send(xb_from.at[dz], xb_recv.at[dz], xb_s.at[dz], xb_r.at[dz], far)

    def xb_wait(*steps):
        for dz in steps:
            xb_copies[dz].wait_recv()

    others(4)
    others(3)
    others(5)
    pl.semaphore_wait(barrier, len(near) + 2)
    for peer in near:
        pl.semaphore_signal(tokens, inc=1, device_id=peer, device_id_type=MESH)
    c0 = send(cgb.at[1 - core], c0buf, c0_s, c0_r, partner)
    for dz in (4, 3, 5):
        send_others(dz)
    for dz in ORDER[3:]:
        others(dz)
        send_others(dz)

    c0.wait_recv()
    cand[...] = jnp.where(root_core == core, cgb[core], c0buf[...])
    cx = send(cand.at[1 - h], cxbuf, cx_s, cx_r, far)

    for dz in (4, 3, 5):
        mine(dz)
        xb_send(dz)
    for unit in range(2):
        relay(unit, 0)
        relay(unit, 1)

    for dz in ORDER[3:]:
        mine(dz)
        xb_send(dz)

    loads[7].wait()
    loads[8].wait()
    wt = (pd[...].astype(F32) * coulomb[...].reshape(1, 512).astype(F32)).astype(BF16)
    r0, p0 = iota((256, 256), 0), iota((256, 256), 1)
    order = one_hot(p0 == (r0 % 8) * 32 + ((r0 // 8) % 8) * 4 + r0 // 64)
    wperm[...] = jnp.dot(order, wt, preferred_element_type=F32).astype(BF16)
    kp = pairs[pl.ds(row, 1), :]
    kc = kp % 32
    target = (kc % 4) * 64 + (kc // 4) * 8 + kp // 32
    perm[...] = one_hot((r0 == target) & (p0 < counts[row]))
    i0 = iota((128, 256), 0)
    for j in range(4):
        pick[j] = one_hot((i0 // 32 == j) & (i0 % 32 == cp % 32))

    relay(0, 2)
    relay(1, 2)
    relay(0, 3)
    relay(1, 3)

    pl.semaphore_wait(tokens, len(near))
    cx.wait_recv()
    quarter[...] = jnp.where(root_h == h, cand[h], cxbuf[...])
    c1 = []
    for i, dz in enumerate(ORDER[:7]):
        zz = (z + dz) % 8
        c1.append(send(quarter.at[zz], c1buf.at[z], c1_s.at[i], c1_r.at[i], at(h, zz, core)))
    c1buf[z] = quarter[z]

    xb_wait(4, 3, 5)
    relay(2, 0)
    relay(2, 1)

    relay(0, 4)
    relay(1, 4)
    relay(0, 5)
    relay(1, 5)

    relay(2, 2)
    xb_wait(2, 6)
    relay(2, 3)

    relay(0, 6)
    relay(1, 6)

    for copy in c1:
        copy.wait_recv()
    colbuf[h, core, z] = c1buf[root_z]
    c2 = []
    for i, (dh, dz) in enumerate(chips):
        slot = colbuf.at[h, core, z]
        c2.append(send(slot, slot, c2_s.at[i], c2_r.at[i], at((h + dh) % 2, (z + dz) % 8, core)))
    c3 = [send(colbuf.at[h, core, z], colbuf.at[h, core, z], c3_s.at[15], c3_r.at[15], partner)]

    relay(2, 4)
    xb_wait(1, 7)
    relay(2, 5)

    for q in range(2):
        xsend[q] = final(0, q).astype(BF16)
    x_copy = send(xsend, xrecv, x_s, x_r, far)
    for q in range(2):
        mine_sum[pl.ds(q * 16, 16), :] = final(1, q)
    relay(2, 6)
    xb_wait(0)
    for q in range(2):
        mine_sum[pl.ds(32 + q * 16, 16), :] = final(2, q)

    loads[6].wait()
    x_copy.wait_recv()
    sv = jnp.concatenate(
        [mine_sum[0:32, :] + xrecv[...].reshape(32, 512).astype(F32), mine_sum[32:64, :]], axis=0
    ).astype(BF16)
    w0, w1 = iota((64, 64), 0), iota((64, 64), 1)
    swap = one_hot(w1 == (w0 % 8) * 8 + w0 // 8)
    sv = jnp.dot(swap, sv, preferred_element_type=F32).astype(BF16)
    dt = dot_t(sv, cond[...]).astype(BF16)
    dt = jnp.concatenate([dt[:, b * 128 : b * 128 + 128] for b in range(8)], axis=0)
    v_of = cp // 32
    for j in range(4):
        e = jnp.dot(dt, pick[j], preferred_element_type=F32).reshape(8, 8, 8, 256)
        total = jnp.where(v_of == 0, e[:, 0], 0.0)
        for v in range(1, 8):
            total = total + jnp.where(v_of == v, e[:, v], 0.0)
        direct[j] = total.reshape(64, 256)

    for i in reversed(range(15)):
        dh, dz = chips[i]
        c2[i].wait_recv()
        slot = colbuf.at[(h + dh) % 2, core, (z + 8 - dz) % 8]
        c3.append(send(slot, slot, c3_s.at[i], c3_r.at[i], partner))
    for copy in c3:
        copy.wait_recv()
    exch = 2.0 * (
        dot_t(wperm[:, 0:256], colbuf[0].reshape(256, 256))
        + dot_t(wperm[:, 256:512], colbuf[1].reshape(256, 256))
    )
    parts = [exch[j * 64 : j * 64 + 64, :] - direct[j] for j in range(4)]
    for d in range(8):
        piece = jnp.concatenate([p[:, d * 32 : d * 32 + 32] for p in parts], axis=1)
        gsend[d] = piece.astype(BF16)
    g_copies = []
    for d in range(1, 8):
        to = (ga + d) % 8
        g_copies.append(
            send(gsend.at[to], grecv.at[d - 1], g_s.at[d - 1], g_r.at[d - 1], {"row": row, "ga": to})
        )
    total = gsend[ga].astype(F32)
    for d, copy in enumerate(g_copies):
        copy.wait_recv()
        total = total + grecv[d].astype(F32)
    total = total.astype(BF16).astype(F32)
    stacked = jnp.concatenate(
        [total if j == 0 else pltpu.roll(total, 128 - 32 * j, 1) for j in range(4)], axis=0
    ).astype(BF16)
    result = dot_l(stacked, perm[...])[0:32]
    slot = ga * 32 + iota((32, 256), 0)
    out_ref[...] = jnp.where(slot < counts[ck], result, 0.0).astype(BF16)
    for copy in sent:
        copy.wait_send()


def per_device(
    pair_dens, cond_dens, val_dens, screened, coulomb, pair_list, counts, q_index, column_k
):
    dma = pltpu.SemaphoreType.DMA
    vmem = pl.BlockSpec(memory_space=pltpu.VMEM)
    hbm = pl.BlockSpec(memory_space=pltpu.HBM)
    return pl.pallas_call(
        kernel,
        out_shape=jax.ShapeDtypeStruct((32, 256), BF16),
        in_specs=[hbm] * 9,
        out_specs=vmem,
        scratch_shapes=[
            pltpu.SMEM((32,), jnp.int32),
            pltpu.SMEM((32,), jnp.int32),
            pltpu.SMEM((1,), jnp.int32),
            pltpu.VMEM((32, 256), jnp.int32),
            pltpu.VMEM((512,), BF16),
            pltpu.VMEM((256, 512), BF16),
            pltpu.VMEM((1024, 512), BF16),
            pltpu.VMEM((32, 64, 128), BF16),
            pltpu.VMEM((8, 512, 128), BF16),
            pltpu.VMEM((8, 2, 64, 512), F32),
            pltpu.VMEM((8, 2, 64, 512), BF16),
            pltpu.VMEM((8, 2, 64, 512), BF16),
            pltpu.VMEM((2, 3, 7, 16, 512), BF16),
            pltpu.VMEM((2, 3, 7, 16, 512), BF16),
            pltpu.VMEM((8, 32, 512), BF16),
            pltpu.VMEM((8, 32, 512), BF16),
            pltpu.VMEM((2, 16, 512), BF16),
            pltpu.VMEM((2, 16, 512), BF16),
            pltpu.VMEM((64, 512), F32),
            pltpu.VMEM((2, 2, 8, 16, 256), BF16),
            pltpu.VMEM((2, 8, 16, 256), BF16),
            pltpu.VMEM((2, 8, 16, 256), BF16),
            pltpu.VMEM((8, 16, 256), BF16),
            pltpu.VMEM((8, 16, 256), BF16),
            pltpu.VMEM((8, 16, 256), BF16),
            pltpu.VMEM((2, 2, 8, 16, 256), BF16),
            pltpu.VMEM((256, 256), BF16),
            pltpu.VMEM((256, 512), BF16),
            pltpu.VMEM((4, 128, 256), BF16),
            pltpu.VMEM((4, 64, 256), F32),
            pltpu.VMEM((8, 64, 128), BF16),
            pltpu.VMEM((7, 64, 128), BF16),
            dma((9,)),
            dma((8,)), dma((8,)),
            dma((2, 3, 7)), dma((2, 3, 7)),
            dma((8,)), dma((8,)),
            dma, dma,
            dma, dma,
            dma, dma,
            dma((7,)), dma((7,)),
            dma((15,)), dma((15,)),
            dma((16,)), dma((16,)),
            dma((7,)), dma((7,)),
            pltpu.SemaphoreType.REGULAR,
        ],
        compiler_params=pltpu.CompilerParams(
            collective_id=0, has_side_effects=True, vmem_limit_bytes=56524800
        ),
        name="bse_block",
    )(
        counts, q_index, column_k, pair_list, coulomb,
        pair_dens, cond_dens, val_dens, screened,
    ).T


def solution(mesh):
    placed = (
        P("row", None, "ga"),
        P("row", None, "ga"),
        P(None, None, "row"),
        P(None, "ga", "row"),
        P("ga"),
        P(),
        P(),
        P(),
        P(),
    )
    return jax.shard_map(
        per_device, mesh=mesh, in_specs=placed, out_specs=P("row", "ga"), check_vma=False
    )
```

time: 48.1 us -> 40.5 us (0.84)
  the two profiles are of different devices: /device:TPU:4 before, /device:TPU:1 now
where the time goes in v2:
time: 40.5 us; the launch traced here: 40.3 us
  Pallas kernels  38.3 us (95%)
  local copies, waits for them, and re-layouts  1.26 us (3%)
  between operations  0.71 us (2%)
    pallas_call x1, Pallas kernels, per_device(): pl.pallas_call(kernel, out_shape=jax.ShapeDtypeStruct((32, 256), BF16), i...  38.3 us
    unnamed x7, local copies, waits for them, and re-layouts  1.26 us

profile of v2, /device:TPU:1, one launch (start us, length us, event | category | flops | bytes accessed | tf_op | source)
XLA Modules:
  0.0 40.3 jit_solution(13879553293852997724)
XLA Ops:
  0.0 0.0 copy-start.1
  0.0 0.0 copy-start
  0.7 0.0 copy-done.1
  0.7 0.0 copy-done
  0.7 0.0 copy-start.2
  0.7 0.6 %copy-done.2 = s32[32]{0:T(128)S(1)} copy-done((s32[32]{0:T(128)S(1)}, s32[32]{0:T(128)}, u32[]{:S(2)}) %copy-start.2) | copy-done | bytes 152
  1.4 38.3 %bse_block.1 = bf16[32,256]{1,0:T(8,128)(2,1)S(1)} custom-call(s32[32]{0:T(128)S(1)} %copy-done.1, s32[32]{0:T(128)S(1)} %copy-done.2, s32[1]{0:T(128)S(6)} %copy.11.column_hbm, s32[32,256]{1,0:T(8,128)} %pairs_hbm.1, bf16[512]{0:T(512)(128)(2,1)S(1)} %copy-done, bf16[1,256,512]{2,1,0:T(8,128)(2,1)} %pd_hbm.1, bf16[1,1024,512]{2,1,0:T(8,128)(2,1)} %cond_hbm.1, ...), custom_call_target="tpu_custom_call" | custom-call | tf_op jit(solution)/shard_map/bse_block/pallas_call | solution.py:311
  39.7 0.6 %copy.12 = bf16[256,32]{0,1:T(8,128)(2,1)} copy(bf16[256,32]{0,1:T(8,128)(2,1)S(1)} %bitcast.1) | data formatting | bytes 32768
Async XLA Ops:
  0.0 0.7 %copy-start.1 = (s32[32]{0:T(128)S(1)}, s32[32]{0:T(128)}, u32[]{:S(2)}) copy-start(s32[32]{0:T(128)} %counts_hbm.1) | copy-start | bytes 388
  0.0 0.7 %copy-start = (bf16[512]{0:T(512)(128)(2,1)S(1)}, bf16[512]{0:T(512)(128)(2,1)}, u32[]{:S(2)}) copy-start(bf16[512]{0:T(512)(128)(2,1)} %coul_hbm.1) | copy-start | bytes 3076
  0.7 0.7 %copy-start.2 = (s32[32]{0:T(128)S(1)}, s32[32]{0:T(128)}, u32[]{:S(2)}) copy-start(s32[32]{0:T(128)} %q_hbm.1) | copy-start | bytes 388
